TPU v7x, 32 devices: a whole 2x2x4 slice. The times are simulated.
32 devices in a mesh: genes: 16 (over z, y, core), cols: 2 (over x).
Axes of the slice: x: 2, y: 2, z: 4, core: 2. Of those that a mesh axis runs over, the one named last changes fastest.
Arguments:
- expression: float32 [384, 40960], P(None, ('genes', 'cols')), may hold values from -200 to 200
- resample: int32 [384], replicated, may hold values from 0 to 383
- labels: int32 [40960, 300], P(('genes', 'cols')), may hold values from 0 to 1, as said below
- ref_kim: float32 [40960], P(('genes', 'cols')), may hold values from 0 to 1
Outputs:
- connectivity: float32 [40960, 300], P(('genes', 'cols'))
- preservation: float32 [2, 300], replicated
Inputs may be any that keep to these rules, and one draw needn't show every extreme that they name: `labels`: each row holds exactly one 1; every module has 32 or more genes.
All inputs are finite; a program needn't handle non-finite values.
Results may differ from a plain program's by a relative error of at most 0.0031.
Values may be sent and summed in bfloat16 or wider, within the bound.
A program may use at most 128 MiB of HBM per device.

v0:
```python
import math

import jax
import jax.numpy as jnp
from jax import lax
from jax.sharding import PartitionSpec as P

G = 40960


def standardize(expression, resample):
    boot = jnp.take(expression, resample, axis=0)
    centered = boot - jnp.mean(boot, axis=0, keepdims=True)
    total = jnp.sum(centered * centered, axis=0, keepdims=True)
    return (centered * lax.rsqrt(total + 1e-06)).astype(jnp.bfloat16)


def local_sums(connectivity, labels, ref_kim):
    member = labels.astype(jnp.float32)
    kim = jnp.sum(connectivity * member, axis=1)
    rowsum = jnp.sum(connectivity, axis=1)
    stacked = jnp.stack(
        [kim, kim * kim, ref_kim, ref_kim * ref_kim, kim * ref_kim, rowsum, jnp.ones_like(kim)],
        axis=1,
    )
    return jnp.dot(
        member.T, stacked, precision=lax.Precision.HIGHEST, preferred_element_type=jnp.float32
    )


def preserve(sums, total_genes):
    counts = sums[:, 6]
    mean_x = sums[:, 0] / (counts * counts)
    var_x = jnp.maximum(sums[:, 1] / (counts * counts * counts) - mean_x * mean_x, 0.0001)
    mean_y = sums[:, 2] / counts
    var_y = jnp.maximum(sums[:, 3] / counts - mean_y * mean_y, 0.01)
    cross = sums[:, 4] / (counts * counts) - mean_x * mean_y
    between = (sums[:, 5] - sums[:, 0]) / (counts * (total_genes - counts))
    density = (mean_x - between) * jnp.sqrt(counts / var_x)
    linked = cross * jnp.sqrt(counts / (var_x * var_y))
    return jnp.stack([density, linked], axis=0)


def tile_term(row_block, column_block, column_ids, module_count):
    scores = lax.dot_general(
        row_block, column_block, (((0,), (0,)), ((), ())), preferred_element_type=jnp.float32
    )
    squares = scores * scores
    adjacency = (squares * squares * squares).astype(jnp.bfloat16)
    member_block = (
        column_ids[:, None] == jnp.arange(module_count, dtype=jnp.int32)[None, :]
    ).astype(jnp.bfloat16)
    return jnp.dot(adjacency, member_block, preferred_element_type=jnp.float32)


def add_tiles(carried, row_block, piece, every_ids, shard_width, module_count):
    span_width = piece.shape[1]
    column_step = shard_width * math.gcd(span_width // shard_width, 8)
    steps_total = span_width // column_step

    def one_step(step_index, accumulated):
        columns = lax.dynamic_slice_in_dim(piece, step_index * column_step, column_step, 1)
        column_ids = lax.dynamic_slice_in_dim(every_ids, step_index * column_step, column_step, 0)
        return accumulated + tile_term(row_block, columns, column_ids, module_count)

    return lax.fori_loop(0, steps_total, one_step, carried)


def local(expression, resample, labels, ref_kim):
    scaled = standardize(expression, resample)
    module_count = labels.shape[1]
    shard_width = scaled.shape[1]
    module_ids = jnp.sum(labels * jnp.arange(module_count, dtype=jnp.int32)[None, :], axis=1)
    row_block = lax.all_gather(scaled, "cols", axis=1, tiled=True)
    panel_ids = lax.all_gather(module_ids, "genes", axis=0, tiled=True)
    initial = jnp.zeros((row_block.shape[1], module_count), jnp.float32)
    partial_value = add_tiles(
        initial,
        row_block,
        lax.all_gather(scaled, "genes", axis=1, tiled=True),
        panel_ids,
        shard_width,
        module_count,
    )
    connectivity = lax.psum_scatter(partial_value, "cols", scatter_dimension=0, tiled=True)
    sums = lax.psum(local_sums(connectivity, labels, ref_kim), ("genes", "cols"))
    return (connectivity, preserve(sums, G))


def solution(mesh):
    placed = (P(None, ("genes", "cols")), P(), P(("genes", "cols"), None), P(("genes", "cols")))
    return jax.shard_map(
        local,
        mesh=mesh,
        in_specs=placed,
        out_specs=(P(("genes", "cols"), None), P()),
        check_vma=False,
    )
```

profile of v0, /device:TPU:0, one launch (start us, length us, event | category | flops | bytes accessed | tf_op | source)
XLA Modules:
  0.0 391.7 jit_solution(1327400909456358095)
XLA Ops:
  7.2 0.0 copy-start
  7.2 0.0 all-gather.6.cloned.1.call-start
  7.2 0.8 compare_select_fusion
  8.0 0.7 compare_and_fusion
  8.7 0.0 copy-done
  8.8 2.7 gather_fusion
  11.5 0.0 copy-start.2
  11.5 1.9 select_reduce_fusion
  13.4 0.2 copy-done.2
  13.6 0.3 multiply_reduce_fusion
  14.0 0.0 copy-start.3
  14.0 1.3 multiply_convert_fusion
  15.2 0.0 all-gather.6.cloned.1.call-update
  15.3 0.0 all-gather.4.cloned.1.call-start
  15.3 0.7 all-gather.4.cloned.1.call-update
  16.0 0.0 reduce-scatter.2.cloned.1.call-start
  16.1 0.0 copy-done.3
  16.1 0.2 multiply_reduce_fusion.2
  16.3 23.3 %all-gather = s32[16,1,1280]{2,1,0:T(1,128)S(1)} all-gather(s32[1,1,1280]{2,1,0:T(1,128)S(1)} %reshape.229), channel_id=1, replica_groups=mesh['genes'=16,'cols'=2] {'genes'}, dimensions={0}, use_global_device_ids=true | all-gather | bytes 87040 | tf_op jit(solution)/shard_map/all_gather | solution.py:75
  39.6 10.2 %all-gather.6.cloned.1.call-done = bf16[384,2560]{1,0:T(8,128)(2,1)} async-done(((bf16[384,1280]{1,0:T(8,128)(2,1)}), bf16[384,2560]{1,0:T(8,128)(2,1)}) %all-gather.6.cloned.1.call-update) | async-done | bytes 1966096 | tf_op jit(solution)/shard_map/all_gather | solution.py:74
  49.8 122.7 %all-gather.4.cloned.1.call-done = bf16[384,20480]{1,0:T(8,128)(2,1)} async-done(((bf16[384,1280]{1,0:T(8,128)(2,1)}), bf16[384,20480]{1,0:T(8,128)(2,1)}) %all-gather.4.cloned.1.call-update) | async-done | bytes 15728656 | tf_op jit(solution)/shard_map/all_gather | solution.py:80
  172.5 124.2 %while.14 = (s32[]{:T(128)}, f32[2560,300]{0,1:T(8,128)}, bf16[384,20480]{1,0:T(8,128)(2,1)}, bf16[384,2560]{1,0:T(8,128)(2,1)}, s32[20480]{0:T(1024)S(1)}, /*index=5*/s32[]{:T(128)}, s32[]{:T(128)}, s32[]{:T(128)}, s32[]{:T(128)}) while((s32[]{:T(128)}, f32[2560,300]{0,1:T(8,128)}, bf16[384,20480]{1,0:T(8,128)(2,1)}, ...), condition=%wide.region_4.5_spmd.clone, body=%wide.region_3.4_spmd.clone.sunk | while | flops 35970764800 | bytes 120955040 | solution.py:66
  172.5 37.4 %fusion.clone.9 = bf16[2560,10240]{0,1:T(8,128)(2,1)} fusion(bf16[384,2560]{1,0:T(8,128)(2,1)} %get-tuple-element.184, bf16[384,20480]{1,0:T(8,128)(2,1)} %get-tuple-element.183, s32[]{:T(128)S(6)} %select_n.27), kind=kOutput, calls=%fused_computation.2.clone.clone.clone.clone.clone.2.clone.1 | convolution fusion | flops 20237516800 | bytes 62259204 | tf_op jit(solution)/shard_map/while/body/eval_jaxpr/dot_general | solution.py:45
  209.9 24.2 %fusion.47 = f32[2560,300]{0,1:T(8,128)} fusion(s32[10240]{0:T(1024)S(1)} %dynamic_slice.28, f32[2560,300]{0,1:T(8,128)} %get-tuple-element.173, pred[]{:T(512)S(6)} %compare.3, bf16[2560,10240]{0,1:T(8,128)(2,1)} %fusion.clone.9), kind=kOutput, calls=%fused_computation.7.clone.3 | convolution fusion | flops 15733248000 | bytes 58613760 | tf_op jit(solution)/shard_map/while/body/eval_jaxpr/dot_general | solution.py:53
  234.1 37.4 %fusion.clone.9 = bf16[2560,10240]{0,1:T(8,128)(2,1)} fusion(bf16[384,2560]{1,0:T(8,128)(2,1)} %get-tuple-element.184, bf16[384,20480]{1,0:T(8,128)(2,1)} %get-tuple-element.183, s32[]{:T(128)S(6)} %select_n.27), kind=kOutput, calls=%fused_computation.2.clone.clone.clone.clone.clone.2.clone.1 | convolution fusion | flops 20237516800 | bytes 62259204 | tf_op jit(solution)/shard_map/while/body/eval_jaxpr/dot_general | solution.py:45
  271.6 25.1 %fusion.47 = f32[2560,300]{0,1:T(8,128)} fusion(s32[10240]{0:T(1024)S(1)} %dynamic_slice.28, f32[2560,300]{0,1:T(8,128)} %get-tuple-element.173, pred[]{:T(512)S(6)} %compare.3, bf16[2560,10240]{0,1:T(8,128)(2,1)} %fusion.clone.9), kind=kOutput, calls=%fused_computation.7.clone.3 | convolution fusion | flops 15733248000 | bytes 58613760 | tf_op jit(solution)/shard_map/while/body/eval_jaxpr/dot_general | solution.py:53
  296.7 0.0 copy-start.5
  296.7 0.0 copy-start.4
  296.7 0.0 reduce-scatter.2.cloned.1.call-update
  296.7 0.7 copy-done.5
  297.4 0.0 copy-start.1
  297.4 40.6 %reduce-scatter.2.cloned.1.call-done = f32[1280,300]{0,1:T(8,128)} async-done(((f32[2560,300]{0,1:T(8,128)}), f32[1280,300]{0,1:T(8,128)}) %reduce-scatter.2.cloned.1.call-update) | async-done | bytes 1536016 | tf_op jit(solution)/shard_map/reduce_scatter | solution.py:85
  338.0 0.0 copy-done.4
  338.0 1.6 fusion.26
  339.7 0.6 stack.27
  340.3 0.6 stack.28
  340.9 0.6 stack_broadcast_in_dim.3
  341.5 1.4 stack.29
  342.9 2.1 fusion.12
  345.0 39.5 %psum.7 = f32[300,7]{0,1:T(8,128)S(1)} all-reduce(f32[300,7]{0,1:T(8,128)S(1)} %fusion.12), channel_id=1, replica_groups=mesh['genes'=16,'cols'=2] {'genes','cols'}, use_global_device_ids=true, to_apply=%region_8.9 | all-reduce | flops 2100 | bytes 16800 | tf_op jit(solution)/shard_map/psum | solution.py:86
  384.6 0.6 pad_maximum_fusion
  385.1 0.0 copy-done.1
  (14 shorter events, 0.1 us)
Async XLA Ops:
  7.2 1.6 copy-start
  7.2 42.6 %all-gather.6.cloned.1.call-start = ((), (), s32[]{:S(2)}) async-start(), calls=%async_computation.2 | async-start | bytes 2949120 | tf_op jit(solution)/shard_map/all_gather | solution.py:74
  11.5 2.1 copy-start.2
  14.0 2.1 copy-start.3
  15.3 157.2 %all-gather.4.cloned.1.call-start = ((), (), s32[]{:S(2)}) async-start(), calls=%async_computation.1 | async-start | bytes 16711680 | tf_op jit(solution)/shard_map/all_gather | solution.py:80
  16.0 322.0 %reduce-scatter.2.cloned.1.call-start = ((), (), s32[]{:S(2)}) async-start(), calls=%async_computation.3 | async-start | bytes 4669440 | tf_op jit(solution)/shard_map/reduce_scatter | solution.py:85
  296.7 0.7 copy-start.5
  296.7 41.4 %copy-start.4 = (s32[1280,300]{0,1:T(8,128)S(1)}, s32[1280,300]{0,1:T(8,128)}, u32[]{:S(2)}) copy-start(s32[1280,300]{0,1:T(8,128)} %param.8) | copy-start | bytes 4608004
  297.4 87.8 %copy-start.1 = (f32[384,1280]{1,0:T(8,128)S(1)}, f32[384,1280]{1,0:T(8,128)}, u32[]{:S(2)}) copy-start(f32[384,1280]{1,0:T(8,128)} %param.6) | copy-start | bytes 5898244
Sparse Core Ops, SparseCore 0:
  15.4 34.3 all-gather.5
  52.6 119.7 all-gather.3
  296.8 41.1 reduce-scatter.1
where the time goes:
time: 392 us
  waiting for transfers between devices  174 us (44%)
  matrix products  126 us (32%)
  blocking collectives  62.8 us (16%)
  between operations  13.9 us (4%)
  other arithmetic  7.47 us (2%)
  local copies, waits for them, and re-layouts  6.83 us (2%)
    all_gather x1, waiting for transfers between devices, local(): lax.all_gather(scaled, 'genes', axis=1, tiled=True)  123 us
    dot_general x2, matrix products, tile_term(): lax.dot_general(row_block, column_block, (((0,), (0,)), ((), ())), prefer...  74.9 us
    dot_general x2, matrix products, tile_term(): return jnp.dot(adjacency, member_block, preferred_element_type=jnp.float32)  49.3 us
    reduce_scatter x1, waiting for transfers between devices, local(): lax.psum_scatter(partial_value, 'cols', scatter_dimension=0, tiled=True)  40.6 us
    psum x1, blocking collectives, local(): lax.psum(local_sums(connectivity, labels, ref_kim), ('genes', 'cols'))  39.5 us
    all_gather x1, blocking collectives, local(): panel_ids = lax.all_gather(module_ids, 'genes', axis=0, tiled=True)  23.3 us
    all_gather x1, waiting for transfers between devices, local(): row_block = lax.all_gather(scaled, 'cols', axis=1, tiled=True)  10.2 us
  transfers between devices with their start and end apart: 3, of which 3 were waited for; matrix products, arithmetic and copies ran while one was open for 0% of the time, Pallas kernels for 0%

commit v1 on v0

v1 whole, which is shorter than its diff:
```python
import functools

import jax
import jax.numpy as jnp
from jax import lax
from jax.experimental import pallas as pl
from jax.experimental.pallas import tpu as pltpu
from jax.sharding import PartitionSpec as P

G = 40960
MESH = pl.DeviceIdType.MESH
ID_LANES = 256
ID_BASE = 16
TILE = 256


def round_up(value, unit):
    return -(-value // unit) * unit


def ring_chip(position, chips):
    half = chips // 2
    return jnp.where(position < half, 2 * position, 2 * (chips - 1 - position) + 1)


def ring_position(chip, chips):
    level = chip // 2
    return jnp.where(lax.rem(chip, 2) == 0, level, chips - 1 - level)


def network_kernel(
    chips, width, block_hbm, rows_hbm, out_ref,
    slots, rows, member, powers, total, outgoing, incoming,
    local_sem, ring_send, ring_recv, pair_send, pair_recv, row_sem, half_sem,
):
    genes_at = lax.axis_index("genes")
    cols_at = lax.axis_index("cols")
    core = lax.rem(genes_at, 2)
    chip = genes_at // 2
    position = ring_position(chip, chips)
    after = lax.rem(position + 1, chips)
    before = lax.rem(position + chips - 1, chips)
    forward = jnp.where(core == 0, after, before)
    backward = jnp.where(core == 0, before, after)
    next_device = (ring_chip(forward, chips) * 2 + core, cols_at)
    last_device = (ring_chip(backward, chips) * 2 + core, cols_at)
    pair_device = (chip * 2 + 1 - core, cols_at)
    side_device = (genes_at, 1 - cols_at)

    load_block = pltpu.make_async_copy(block_hbm, slots.at[0], local_sem.at[0])
    load_rows = pltpu.make_async_copy(rows_hbm, rows.at[0], local_sem.at[1])
    load_block.start()
    load_rows.start()
    barrier = pltpu.get_barrier_semaphore()
    for device in (next_device, last_device, pair_device, side_device):
        pl.semaphore_signal(barrier, inc=1, device_id=device, device_id_type=MESH)
    total[...] = jnp.zeros_like(total)
    load_block.wait()
    load_rows.wait()
    pl.semaphore_wait(barrier, 4)

    def ring_copy(step):
        return pltpu.make_async_remote_copy(
            src_ref=slots.at[2 * step], dst_ref=slots.at[2 * step + 2],
            send_sem=ring_send.at[step], recv_sem=ring_recv.at[step],
            device_id=next_device, device_id_type=MESH,
        )

    def pair_copy(step):
        return pltpu.make_async_remote_copy(
            src_ref=slots.at[2 * step], dst_ref=slots.at[2 * step + 1],
            send_sem=pair_send.at[step], recv_sem=pair_recv.at[step],
            device_id=pair_device, device_id_type=MESH,
        )

    row_copy = pltpu.make_async_remote_copy(
        src_ref=rows.at[0], dst_ref=rows.at[1],
        send_sem=row_sem.at[0], recv_sem=row_sem.at[1],
        device_id=side_device, device_id_type=MESH,
    )

    modules = member.shape[0]
    id_rows = -(-width // ID_LANES)
    tile = TILE if width % TILE == 0 else width

    def set_members(slot):
        coded = slots[slot, width:, :ID_LANES].astype(jnp.float32)
        names = lax.broadcasted_iota(jnp.int32, (modules, ID_LANES), 0).astype(jnp.float32)
        for row in range(id_rows):
            ids = coded[row : row + 1] * ID_BASE + coded[id_rows + row : id_rows + row + 1]
            lanes = min(ID_LANES, width - row * ID_LANES)
            hit = jnp.where(names == ids, 1.0, 0.0).astype(jnp.bfloat16)
            member[:, row * ID_LANES : row * ID_LANES + lanes] = hit[:, :lanes]

    def add_block(slot, halves):
        set_members(slot)

        def one_tile(index, carry):
            spot = pl.ds(pl.multiple_of(index * tile, tile), tile)
            for half in halves:
                scores = lax.dot_general(
                    slots[slot, :width, :], rows[half, spot, :], (((1,), (1,)), ((), ())),
                    preferred_element_type=jnp.float32,
                )
                squares = scores * scores
                powers[half] = (squares * squares * squares).astype(jnp.bfloat16)
            for half in halves:
                total[half, :, spot] += jnp.dot(
                    member[:, :width], powers[half], preferred_element_type=jnp.float32
                )
            return carry

        lax.fori_loop(0, width // tile, one_tile, 0)

    ring_copy(0).start()
    pair_copy(0).start()
    row_copy.start()
    add_block(0, (0,))
    pair_copy(0).wait_recv()
    add_block(1, (0,))
    row_copy.wait_recv()

    def early(slot, carry):
        add_block(slot, (1,))
        return carry

    lax.fori_loop(0, 2, early, 0)

    def one_step(step, carry):
        ring_copy(step - 1).wait_recv()
        ring_copy(step).start()
        pair_copy(step).start()
        add_block(2 * step, (0, 1))
        pair_copy(step).wait_recv()
        add_block(2 * step + 1, (0, 1))
        return carry

    lax.fori_loop(1, chips - 1, one_step, 0)

    end = chips - 1
    ring_copy(end - 1).wait_recv()
    pair_copy(end).start()
    add_block(2 * end, (1,))
    pair_copy(end).wait_recv()
    add_block(2 * end + 1, (1,))
    outgoing[...] = total[1, :, :width].astype(jnp.bfloat16)
    half_copy = pltpu.make_async_remote_copy(
        src_ref=outgoing, dst_ref=incoming,
        send_sem=half_sem.at[0], recv_sem=half_sem.at[1],
        device_id=side_device, device_id_type=MESH,
    )
    half_copy.start()

    def late(index, carry):
        add_block(2 * end + index, (0,))
        return carry

    lax.fori_loop(0, 2, late, 0)

    def drain(step, carry):
        ring_copy(step).wait_send()
        pair_copy(step).wait_send()
        return carry

    lax.fori_loop(0, end, drain, 0)
    pair_copy(end).wait_send()
    row_copy.wait_send()
    half_copy.wait()
    out_ref[...] = total[0, :, :width] + incoming[...].astype(jnp.float32)


def network(block, rows, chips, module_rows, collective_id):
    width, depth = rows.shape
    padded = round_up(width, 128)
    dma = pltpu.SemaphoreType.DMA
    return pl.pallas_call(
        functools.partial(network_kernel, chips, width),
        out_shape=jax.ShapeDtypeStruct((module_rows, width), jnp.float32),
        in_specs=[pl.BlockSpec(memory_space=pl.ANY)] * 2,
        out_specs=pl.BlockSpec(memory_space=pltpu.VMEM),
        scratch_shapes=[
            pltpu.VMEM((2 * chips, block.shape[0], depth), jnp.bfloat16),
            pltpu.VMEM((2, width, depth), jnp.bfloat16),
            pltpu.VMEM((module_rows, padded), jnp.bfloat16),
            pltpu.VMEM((2, width, TILE if width % TILE == 0 else width), jnp.bfloat16),
            pltpu.VMEM((2, module_rows, padded), jnp.float32),
            pltpu.VMEM((module_rows, width), jnp.bfloat16),
            pltpu.VMEM((module_rows, width), jnp.bfloat16),
            dma((2,)), dma((chips,)), dma((chips,)), dma((chips,)), dma((chips,)),
            dma((2,)), dma((2,)),
        ],
        compiler_params=pltpu.CompilerParams(
            collective_id=collective_id, has_side_effects=True, vmem_limit_bytes=60 * 1024 * 1024
        ),
    )(block, rows)


def total_kernel(stages, value_ref, out_ref, parts, send_sem, recv_sem):
    genes_at = lax.axis_index("genes")
    cols_at = lax.axis_index("cols")

    def peer(stage, offset):
        axis, stride, count = stage
        if axis == "cols":
            return (genes_at, lax.rem(cols_at + offset, count))
        digit = lax.rem(genes_at // stride, count)
        return (genes_at + (lax.rem(digit + offset, count) - digit) * stride, cols_at)

    barrier = pltpu.get_barrier_semaphore()
    peers = 0
    for stage in stages:
        for offset in range(1, stage[2]):
            pl.semaphore_signal(barrier, inc=1, device_id=peer(stage, offset), device_id_type=MESH)
            peers += 1
    pl.semaphore_wait(barrier, peers)
    base = 0
    current = value_ref[...]
    for stage in stages:
        parts[base] = current
        copies = []
        for offset in range(1, stage[2]):
            copies.append(pltpu.make_async_remote_copy(
                src_ref=parts.at[base], dst_ref=parts.at[base + offset],
                send_sem=send_sem.at[base + offset], recv_sem=recv_sem.at[base + offset],
                device_id=peer(stage, offset), device_id_type=MESH,
            ))
            copies[-1].start()
        for copy in copies:
            copy.wait()
        digit = cols_at if stage[0] == "cols" else lax.rem(genes_at // stage[1], stage[2])
        count = stage[2]
        current = parts[base + lax.rem(digit, count)]
        for origin in range(1, count):
            current = current + parts[base + lax.rem(digit - origin + count, count)]
        base += count
    out_ref[...] = current


def total_sum(value, stages, collective_id):
    slots = sum(stage[2] for stage in stages)
    return pl.pallas_call(
        functools.partial(total_kernel, stages),
        out_shape=jax.ShapeDtypeStruct(value.shape, value.dtype),
        in_specs=[pl.BlockSpec(memory_space=pltpu.VMEM)],
        out_specs=pl.BlockSpec(memory_space=pltpu.VMEM),
        scratch_shapes=[
            pltpu.VMEM((slots,) + value.shape, value.dtype),
            pltpu.SemaphoreType.DMA((slots,)),
            pltpu.SemaphoreType.DMA((slots,)),
        ],
        compiler_params=pltpu.CompilerParams(collective_id=collective_id, has_side_effects=True),
    )(value)


def preserve(sums, total_genes):
    counts = sums[6]
    mean_x = sums[0] / (counts * counts)
    var_x = jnp.maximum(sums[1] / (counts * counts * counts) - mean_x * mean_x, 0.0001)
    mean_y = sums[2] / counts
    var_y = jnp.maximum(sums[3] / counts - mean_y * mean_y, 0.01)
    cross = sums[4] / (counts * counts) - mean_x * mean_y
    between = (sums[5] - sums[0]) / (counts * (total_genes - counts))
    density = (mean_x - between) * jnp.sqrt(counts / var_x)
    linked = cross * jnp.sqrt(counts / (var_x * var_y))
    return jnp.stack([density, linked], axis=0)


def local(genes_size, cols_size, expression, resample, labels, ref_kim):
    samples, width = expression.shape
    module_count = labels.shape[1]
    module_rows = round_up(module_count, 16)
    chips = genes_size // 2
    sample_ids = jnp.arange(samples, dtype=jnp.int32)
    counts = jnp.sum(
        (resample[:, None] == sample_ids[None, :]).astype(jnp.float32), axis=0
    )
    weights = counts[:, None]
    mean = jnp.sum(expression * weights, axis=0, keepdims=True) / resample.shape[0]
    centered = expression - mean
    spread = jnp.sum(centered * centered * weights, axis=0, keepdims=True)
    scaled = (centered * lax.rsqrt(spread + 1e-06)).astype(jnp.bfloat16)
    module_ids = jnp.sum(labels * jnp.arange(module_count, dtype=jnp.int32)[None, :], axis=1)

    id_rows = -(-width // ID_LANES)
    coded = jnp.pad(module_ids, (0, id_rows * ID_LANES - width)).reshape(id_rows, ID_LANES)
    coded = jnp.concatenate([coded // ID_BASE, lax.rem(coded, ID_BASE)], axis=0)
    block_rows = round_up(width + 2 * id_rows, 16)
    coded = jnp.pad(
        coded.astype(jnp.bfloat16), ((0, block_rows - width - 2 * id_rows), (0, 0))
    )
    drawn = counts > 0
    place = jnp.cumsum(drawn.astype(jnp.int32)) - 1

    def at_depth(depth, collective_id):
        def run(_):
            kept = (place[None, :] == jnp.arange(depth, dtype=jnp.int32)[:, None]) & drawn[None, :]
            kept_bf = kept.astype(jnp.bfloat16)
            packed = lax.dot_general(
                scaled, kept_bf, (((0,), (1,)), ((), ())), preferred_element_type=jnp.float32
            )
            kept_counts = jnp.sum(jnp.where(kept, counts[None, :], 0.0), axis=1)
            rows = (packed * kept_counts[None, :]).astype(jnp.bfloat16)
            tail = jnp.pad(coded, ((0, 0), (0, depth - ID_LANES)))
            block = jnp.concatenate([packed.astype(jnp.bfloat16), tail], axis=0)
            return network(block, rows, chips, module_rows, collective_id)

        return run

    short = 256
    distinct = jnp.sum(drawn.astype(jnp.int32))
    if samples > short:
        by_module = lax.cond(
            distinct <= short, at_depth(short, 1), at_depth(round_up(samples, 128), 2), 0
        )
    else:
        by_module = at_depth(short, 1)(0)

    by_module = by_module[:module_count]
    connectivity = by_module.T
    member = (
        jnp.arange(module_count, dtype=jnp.int32)[:, None] == module_ids[None, :]
    ).astype(jnp.float32)
    kim = jnp.sum(by_module * member, axis=0)
    rowsum = jnp.sum(by_module, axis=0)
    stacked = jnp.stack(
        [kim, kim * kim, ref_kim, ref_kim * ref_kim, kim * ref_kim, rowsum,
         jnp.ones_like(kim), jnp.zeros_like(kim)],
        axis=0,
    )
    sums = lax.dot_general(
        stacked, member, (((1,), (1,)), ((), ())),
        precision=lax.Precision.HIGHEST, preferred_element_type=jnp.float32,
    )
    sums = jnp.pad(sums, ((0, 0), (0, round_up(module_count, 128) - module_count)))
    stages = (("genes", 1, 2), ("cols", 1, cols_size), ("genes", 2, 2), ("genes", 4, genes_size // 4))
    sums = total_sum(sums, stages, 3)[:, :module_count]
    return (connectivity, preserve(sums, G))


def solution(mesh):
    placed = (P(None, ("genes", "cols")), P(), P(("genes", "cols"), None), P(("genes", "cols")))
    return jax.shard_map(
        functools.partial(local, mesh.shape["genes"], mesh.shape["cols"]),
        mesh=mesh,
        in_specs=placed,
        out_specs=(P(("genes", "cols"), None), P()),
        check_vma=False,
    )
```

time: 392 us -> 144 us (0.37)
  waiting for transfers between devices: 174 us -> 0 us
  Pallas kernels: 0 us -> 127 us
  matrix products: 126 us -> 2.16 us
  blocking collectives: 62.8 us -> 0 us
  between operations: 13.9 us -> 1.46 us
  local copies, waits for them, and re-layouts: 6.83 us -> 2.58 us
    all_gather x2 -> x0, waiting for transfers between devices: 133 us -> none  [the longest x1 123 us: local(): lax.all_gather(scaled, 'genes', axis=1, tiled=True)]
    pallas_call x0 -> x2, Pallas kernels: none -> 127 us  [the longest x1 113 us: network(): pl.pallas_call(functools.partial(network_kernel, chips, width), out_shape...]
    dot_general x5 -> x2, matrix products: 126 us -> 2.16 us  [the longest x1 1.44 us: run(): lax.dot_general(scaled, kept_bf, (((0,), (1,)), ((), ())), preferred_elem...]
    reduce_scatter x1 -> x0, waiting for transfers between devices: 40.6 us -> none  [local(): lax.psum_scatter(partial_value, 'cols', scatter_dimension=0, tiled=True)]
    psum x1 -> x0, blocking collectives: 39.5 us -> none  [local(): lax.psum(local_sums(connectivity, labels, ref_kim), ('genes', 'cols'))]
    all_gather x1 -> x0, blocking collectives: 23.3 us -> none  [local(): panel_ids = lax.all_gather(module_ids, 'genes', axis=0, tiled=True)]
  transfers between devices with their start and end apart: 3 -> 0, of which waited for: 3 -> 0; matrix products, arithmetic and copies ran while one was open for 0% -> 0% of each run, Pallas kernels for 0% -> 0%
where the time goes in v1:
time: 144 us; the launch traced here: 143 us
  Pallas kernels  127 us (88%)
  other arithmetic  9.7 us (7%)
  local copies, waits for them, and re-layouts  2.58 us (2%)
  matrix products  2.16 us (2%)
  between operations  1.46 us (1%)
    pallas_call x1, Pallas kernels, network(): pl.pallas_call(functools.partial(network_kernel, chips, width), out_shape...  113 us
    pallas_call x1, Pallas kernels, total_sum(): pl.pallas_call(functools.partial(total_kernel, stages), out_shape=jax.Sha...  14.1 us

profile of v1, /device:TPU:0, one launch (start us, length us, event | category | flops | bytes accessed | tf_op | source)
XLA Modules:
  0.0 143.4 jit_solution(16380409241946115453)
XLA Ops:
  0.6 0.0 copy-start
  0.6 1.0 convert_reduce_fusion
  1.6 1.8 %multiply_reduce_fusion.1 = f32[1280]{0:T(1024)S(1)} fusion(f32[384,1280]{1,0:T(8,128)} %param.6, f32[384]{0:T(512)S(1)} %convert_reduce_fusion), kind=kLoop, calls=%fused_computation.30 | loop fusion | flops 981760 | bytes 1972736 | tf_op jit(solution)/shard_map/reduce_sum | solution.py:278
  3.4 0.0 copy-done
  3.4 0.3 multiply_reduce_fusion
  3.7 0.0 copy-start.2
  3.7 0.2 multiply_convert_fusion.2
  3.9 1.2 copy-done.2
  5.1 0.2 multiply_reduce_fusion.2
  5.3 0.3 reduce-window.9
  5.6 0.1 slice.52
  5.7 0.6 convert_reduce_fusion.1
  7.0 117.6 %conditional.1 = (f32[300,1280]{1,0:T(8,128)S(1)}, f32[1,1280]{1,0:T(1,128)S(1)}) conditional(s32[]{:T(128)} %convert_element_type.55, (s32[4,1]{1,0:T(4,128)S(1)}, s32[3,128]{1,0:T(4,128)S(1)}, pred[384]{0:T(512)(128)(4,1)S(1)}, bf16[384,1280]{1,0:T(8,128)(2,1)S(1)}, bf16[10,256]{1,0:T(8,128)(2,1)S(1)}, /*index=5*/f32[384]{0:T(512)S(1)}) %tuple.33, ...), branch_computations={%region_7.10_spmd, %region_10.13_spmd} | conditional | flops 383215744 | bytes 8031572 | solution.py:312
  7.2 0.1 copy.17
  7.3 0.1 add_bitcast_fusion.1
  7.4 0.2 select_reduce_fusion.1
  7.5 1.4 %fusion.10 = (bf16[1280,256]{1,0:T(8,128)(2,1)}, bf16[1280,256]{1,0:T(8,128)(2,1)S(1)}) fusion(f32[256]{0:T(256)S(1)} %select_reduce_fusion.1, bf16[384,1280]{1,0:T(8,128)(2,1)S(1)} %get-tuple-element.86, s32[384]{0:T(512)S(1)} %add_bitcast_fusion.1, pred[384]{0:T(512)(128)(4,1)S(1)} %get-tuple-element.85), kind=kOutput, calls=%fused_computation.18 | convolution fusion | flops 252837888 | bytes 2296704 | tf_op jit(solution)/shard_map/cond/branch_1_fun/dot_general | solution.py:298
  9.0 0.9 fusion.9.block_hbm
  9.9 113.1 %branch_1_fun.2 = f32[304,1280]{1,0:T(8,128)} custom-call(bf16[1296,256]{1,0:T(8,128)(2,1)} %fusion.9.block_hbm, bf16[1280,256]{1,0:T(8,128)(2,1)} %get-tuple-element.130.rows_hbm), custom_call_target="tpu_custom_call" | custom-call | tf_op jit(solution)/shard_map/cond/branch_1_fun/pallas_call | solution.py:176
  123.0 1.6 %fusion.24 = (f32[1280]{0:T(1024)S(1)}, f32[300,1280]{1,0:T(8,128)S(1)}) fusion(f32[304,1280]{1,0:T(8,128)} %branch_1_fun.2), kind=kLoop, calls=%fused_computation.63 | loop fusion | flops 382720 | bytes 3077120 | tf_op jit(solution)/shard_map/reduce_sum | solution.py:324
  124.6 0.0 copy-start.1
  124.6 0.0 copy-start.3
  124.6 0.3 select_reduce_fusion.2
  124.9 0.4 copy-done.3
  125.4 0.1 stack.34
  125.5 0.7 fusion.16
  126.2 0.7 pad.19.value_ref
  126.9 14.1 %shard_map.59 = f32[8,384]{1,0:T(8,128)} custom-call(f32[8,384]{1,0:T(8,128)} %pad.19.value_ref), custom_call_target="tpu_custom_call" | custom-call | tf_op jit(solution)/shard_map/pallas_call | solution.py:241
  141.0 0.9 sqrt_multiply_fusion.1
  141.9 0.9 sqrt_multiply_fusion
  142.8 0.6 pad_maximum_fusion.1
  143.4 0.0 copy-done.1
  (17 shorter events, 0.1 us)
Async XLA Ops:
  0.6 2.7 %copy-start = (f32[384,1280]{1,0:T(8,128)S(1)}, f32[384,1280]{1,0:T(8,128)}, u32[]{:S(2)}) copy-start(f32[384,1280]{1,0:T(8,128)} %param.6) | copy-start | bytes 5898244
  3.7 1.4 copy-start.2
  124.6 18.8 %copy-start.1 = (f32[300,1280]{1,0:T(8,128)}, f32[300,1280]{1,0:T(8,128)S(1)}, u32[]{:S(2)}) copy-start(f32[300,1280]{1,0:T(8,128)S(1)} %get-tuple-element.93) | copy-start | bytes 4608004
  124.6 0.7 copy-start.3
